TPU v7x, 8 devices: a whole 2x2x1 slice. The times are simulated.
8 devices in a mesh: data: 1 (over z), store: 2 (over y), model: 4 (over x, core).
Axes of the slice: x: 2, y: 2, z: 1, core: 2. Of those that a mesh axis runs over, the one named last changes fastest.
Arguments:
- queries: bfloat16 [64, 2048], P('data')
- w_head: bfloat16 [2048, 256000], P(None, 'model')
- store_keys: bfloat16 [65536, 2048], P(('store', 'model'))
- store_tok: int32 [65536], P(('store', 'model'))
- temperature: float32 [], replicated
- mix_weight: float32 [], replicated
Outputs:
- output: float32 [64, 256000], P(('data', 'store'), 'model')
All inputs are finite; a program needn't handle non-finite values.
Results may differ from a plain program's by a relative error of at most 0.001.
Values are sent between devices in bfloat16 or wider.
A program may use at most 1.25 GiB of HBM per device.

v0:
```python
import functools

import jax
import jax.numpy as jnp
from jax import lax
from jax.experimental import pallas as pl
from jax.experimental.pallas import tpu as pltpu
from jax.sharding import PartitionSpec as P

MESH = pl.DeviceIdType.MESH
F32, BF16, I32 = jnp.float32, jnp.bfloat16, jnp.int32
VLIM = 60 * 1024 * 1024
CHUNK = 32


def iota(shape, dim):
    return lax.broadcasted_iota(I32, shape, dim)


def sort_rows(x):
    n = x.shape[0] * 128
    pos = iota(x.shape, 0) * 128 + iota(x.shape, 1)
    k = 2
    while k <= n:
        j = k // 2
        while j >= 1:
            if j >= 128:
                ahead, behind = pltpu.roll(x, 64 - j // 128, 0), pltpu.roll(x, j // 128, 0)
            else:
                ahead, behind = pltpu.roll(x, 128 - j, 1), pltpu.roll(x, j, 1)
            first = (pos & j) == 0
            other = jnp.where(first, ahead, behind)
            low = ((pos & k) == 0) == first
            x = jnp.where(low, jnp.minimum(x, other), jnp.maximum(x, other))
            j //= 2
        k *= 2
    return x


def score_kernel(qt_ref, keys_ref, tok_ref, tau_ref, e_ref, tok_out, start_out, stat_out, s_ref, top_ref, perm_v, perm_s, hot_a, hot_b, rows_ref, sem):
    step, steps = pl.program_id(0), pl.num_programs(0)
    kb = keys_ref.shape[0]
    sub = 256

    @pl.when(step == 0)
    def _():
        top_ref[...] = jnp.full_like(top_ref, -jnp.inf)
        tok = tok_ref[...]
        packed = sort_rows(tok * 8192 + (iota((64, 128), 0) * 128 + iota((64, 128), 1)))
        tok_out[...] = packed >> 13
        perm_v[...] = packed & 8191
        cp = pltpu.make_async_copy(perm_v, perm_s, sem)
        cp.start()
        for r in range(64):
            tile = tok_ref[r : r + 1, :] >> 8
            lanes = slice(r * 128, (r + 1) * 128)
            hot_a[:, lanes] = jnp.where(iota((32, 128), 0) == (tile >> 5), 1.0, 0.0).astype(BF16)
            hot_b[:, lanes] = jnp.where(iota((128, 128), 0) == (tile & 31), 1.0, 0.0).astype(BF16)
        cnt = lax.dot_general(hot_a[...], hot_b[...], (((1,), (1,)), ((), ())), preferred_element_type=F32)
        inc = cnt
        for sh in (1, 2, 4, 8, 16):
            inc = inc + jnp.where(iota((32, 128), 1) >= sh, pltpu.roll(inc, sh, 1), 0.0)
        tot = jnp.broadcast_to(jnp.sum(cnt, axis=1, keepdims=True), (32, 128))
        rp = tot
        for sh in (1, 2, 4, 8, 16):
            rp = rp + jnp.where(iota((32, 128), 0) >= sh, pltpu.roll(rp, sh, 0), 0.0)
        start_out[...] = ((inc - cnt) + (rp - tot)).astype(I32)
        cp.wait()

    def score(i, _):
        at = pl.multiple_of(i * sub, sub)
        kv = keys_ref[pl.ds(at, sub), :]
        dots = jnp.dot(kv, qt_ref[...], preferred_element_type=F32)
        kf = kv.astype(F32)
        norm = jnp.sum(kf * kf, axis=1, keepdims=True)
        s = (2.0 * dots - norm) / tau_ref[0, 0]
        s_ref[pl.ds(pl.multiple_of(step * kb + at, sub), sub), :] = s
        top_ref[...] = jnp.maximum(top_ref[...], jnp.max(s.reshape(sub // 8, 8, 128), axis=0))
        return 0

    lax.fori_loop(0, kb // sub, score, 0)

    @pl.when(step == steps - 1)
    def _():
        top = jnp.max(top_ref[...], axis=0, keepdims=True)

        def block(b, total):
            for u in range(128):
                rows_ref[u : u + 1, :] = s_ref[pl.ds(perm_s[b, u], 1), :]
            x = jnp.exp(rows_ref[...] - top)
            total = total + jnp.sum(x.reshape(16, 8, 128), axis=0)
            xt = x.T
            lanes = pl.ds(pl.multiple_of(b * 128, 128), 128)
            for g in range(8):
                e_ref[g // 4, g % 4, :, lanes] = xt[8 * g : 8 * g + 8, :]
            return total

        total = lax.fori_loop(0, 64, block, jnp.zeros((8, 128), F32))
        total = jnp.sum(total, axis=0, keepdims=True)
        mt = jnp.broadcast_to(top, (128, 128)).T
        zt = jnp.broadcast_to(total, (128, 128)).T
        for s in range(2):
            stat_out[s, 0] = mt[32 * s : 32 * s + 32]
            stat_out[s, 1] = zt[32 * s : 32 * s + 32]


def scores(qt, keys, tok, tau, kb=1024):
    n = keys.shape[0]
    whole = lambda *s: pl.BlockSpec(s, lambda i: (0,) * len(s))
    return pl.pallas_call(
        score_kernel,
        grid=(n // kb,),
        in_specs=[whole(2048, 128), pl.BlockSpec((kb, 2048), lambda i: (i, 0)), whole(64, 128), pl.BlockSpec(memory_space=pltpu.SMEM)],
        out_specs=[whole(2, 4, 8, n), whole(64, 128), whole(32, 128), whole(2, 2, 32, 128)],
        out_shape=[jax.ShapeDtypeStruct((2, 4, 8, n), F32), jax.ShapeDtypeStruct((64, 128), I32), jax.ShapeDtypeStruct((32, 128), I32), jax.ShapeDtypeStruct((2, 2, 32, 128), F32)],
        scratch_shapes=[
            pltpu.VMEM((n, 128), F32), pltpu.VMEM((8, 128), F32), pltpu.VMEM((64, 128), I32), pltpu.SMEM((64, 128), I32),
            pltpu.VMEM((32, n), BF16), pltpu.VMEM((128, n), BF16), pltpu.VMEM((128, 128), F32), pltpu.SemaphoreType.DMA,
        ],
        compiler_params=pltpu.CompilerParams(vmem_limit_bytes=VLIM),
        name="scores",
    )(qt, keys, tok, tau)


def peers():
    s, m = lax.axis_index("store"), lax.axis_index("model")
    x, c = m // 2, m % 2
    return s, m, 1 - s, (1 - x) * 2 + c, x * 2 + (1 - c)


def remote(src, dst, ss, rs, s, m):
    return pltpu.make_async_remote_copy(src_ref=src, dst_ref=dst, send_sem=ss, recv_sem=rs, device_id=(0, s, m), device_id_type=MESH)


def exchange_kernel(e_ref, tok_ref, start_ref, stat_ref, e_all, tok_all, start_all, stat_all, es, er, ps, pr, ts, tr):
    s, m, so, mx, mc = peers()
    me = s * 4 + m
    barrier = pltpu.get_barrier_semaphore()
    for j in range(1, 8):
        d = lax.rem(me + j, 8)
        pl.semaphore_signal(barrier, inc=1, device_id=(0, d // 4, lax.rem(d, 4)), device_id_type=MESH)
    pl.semaphore_wait(barrier, 7)

    small = []
    for j in range(1, 8):
        d = lax.rem(me + j, 8)
        ds_, dm = d // 4, lax.rem(d, 4)
        for k, (a, b) in enumerate(((tok_ref, tok_all.at[me]), (start_ref, start_all.at[me]), (stat_ref.at[ds_], stat_all.at[me]))):
            small.append(remote(a, b, ts.at[j, k], tr.at[j, k], ds_, dm))
    for c in small:
        c.start()
    far = []
    for r in range(4):
        far.append([
            remote(e_ref.at[so, r], e_all.at[me, r], es.at[0, r], er.at[0, r], so, mx),
            remote(e_ref.at[s, r], e_all.at[me, r], es.at[1, r], er.at[1, r], s, mx),
            remote(e_ref.at[so, r], e_all.at[me, r], es.at[2, r], er.at[2, r], so, m),
        ])
        for c in far[-1]:
            c.start()
    own = [remote(e_ref.at[s, r], e_all.at[me, r], ps.at[3, r], pr.at[3, r], s, mc) for r in range(4)]
    for c in own:
        c.start()
    came = (so * 4 + mx, s * 4 + mx, so * 4 + m)
    fwd = []
    for r in range(4):
        for k in (1, 2, 0):
            far[r][k].wait_recv()
            f = remote(e_all.at[came[k], r], e_all.at[came[k], r], ps.at[k, r], pr.at[k, r], s, mc)
            f.start()
            fwd.append(f)
    for c in own + fwd:
        c.wait()
    for r in range(4):
        for c in far[r]:
            c.wait_send()
    for c in small:
        c.wait()


def exchange(e, tok, start, stat):
    n = e.shape[-1]
    anyspec = pl.BlockSpec(memory_space=pl.ANY)
    return pl.pallas_call(
        exchange_kernel,
        in_specs=[anyspec] * 4,
        out_specs=[anyspec] * 4,
        out_shape=[jax.ShapeDtypeStruct((8, 4, 8, n), F32), jax.ShapeDtypeStruct((8, 64, 128), I32), jax.ShapeDtypeStruct((8, 32, 128), I32), jax.ShapeDtypeStruct((8, 2, 32, 128), F32)],
        scratch_shapes=[
            pltpu.SemaphoreType.DMA((3, 4)), pltpu.SemaphoreType.DMA((3, 4)), pltpu.SemaphoreType.DMA((4, 4)), pltpu.SemaphoreType.DMA((4, 4)),
            pltpu.SemaphoreType.DMA((8, 3)), pltpu.SemaphoreType.DMA((8, 3)),
        ],
        compiler_params=pltpu.CompilerParams(collective_id=0, has_side_effects=True),
        name="exchange",
    )(e, tok, start, stat)


def piece(e_ref, tok_ref, scale, starts, ends, base):
    lane = iota((32, 128), 1)
    lane1 = iota((1, 128), 1)
    halves, toks = [], []
    for h in range(2):
        acc, tacc = None, None
        for i in range(4):
            d = 4 * h + i
            at = starts[d]
            row, off = jnp.minimum(at >> 7, 63), at & 127
            nxt = jnp.minimum(row + 1, 63)
            v0 = e_ref[d, :, pl.ds(pl.multiple_of(row * 128, 128), 128)]
            v1 = e_ref[d, :, pl.ds(pl.multiple_of(nxt * 128, 128), 128)]
            sh = (CHUNK * i - off) & 127
            v = pltpu.roll(jnp.where(lane >= off, v0, v1), sh, 1)
            t0, t1 = tok_ref[d, pl.ds(row, 1), :], tok_ref[d, pl.ds(nxt, 1), :]
            t = pltpu.roll(jnp.where(lane1 >= off, t0, t1), sh, 1)
            t = jnp.where(lane1 - CHUNK * i < ends[d] - at, t, -1)
            if i == 0:
                acc, tacc = v, t
            else:
                acc = jnp.where(lane >= CHUNK * i, v, acc)
                tacc = jnp.where(lane1 >= CHUNK * i, t, tacc)
        halves.append(acc)
        toks.append(tacc)
    e = jnp.concatenate(halves, axis=1) * scale
    tok = jnp.concatenate(toks, axis=1) - base
    hi = e.astype(BF16)
    rest = e - hi.astype(F32)
    mid = rest.astype(BF16)
    low = (rest - mid.astype(F32)).astype(BF16)
    lhs = jnp.concatenate([hi, mid, low], axis=0)
    hot = jnp.where(iota((256, 256), 0) == tok, 1.0, 0.0).astype(BF16)
    out = lax.dot_general(lhs, hot, (((1,), (1,)), ((), ())), preferred_element_type=F32)
    return out[0:32] + out[32:64] + out[64:96]


def head_hist_kernel(per, start_s, base_s, q_ref, w_ref, e_ref, tok_ref, scale_ref, logit_ref, hist_ref, stat_ref, top_ref, sum_ref):
    step, steps = pl.program_id(0), pl.num_programs(0)

    @pl.when(step == 0)
    def _():
        top_ref[...] = jnp.full_like(top_ref, -jnp.inf)
        sum_ref[...] = jnp.zeros_like(sum_ref)

    logits = jnp.dot(q_ref[...], w_ref[...], preferred_element_type=F32)
    logit_ref[...] = logits
    old = top_ref[...]
    new = jnp.maximum(old, jnp.max(logits, axis=1, keepdims=True))
    sum_ref[...] = sum_ref[...] * jnp.exp(old - new) + jnp.sum(jnp.exp(logits - new[:, 0:1]), axis=1, keepdims=True)
    top_ref[...] = new
    scale = scale_ref[...]
    for i in range(per):
        t = step * per + i
        starts = [start_s[d, t] for d in range(8)]
        ends = [start_s[d, t + 1] for d in range(8)]
        base = base_s[0] + t * 256
        cols = slice(i * 256, (i + 1) * 256)
        hist_ref[:, cols] = piece(e_ref, tok_ref, scale, starts, ends, base)
        most = functools.reduce(jnp.maximum, [b - a for a, b in zip(starts, ends)])

        @pl.when(most > CHUNK)
        def _():
            def more(it, _):
                at = [jnp.minimum(a + it * CHUNK, b) for a, b in zip(starts, ends)]
                hist_ref[:, cols] += piece(e_ref, tok_ref, scale, at, ends, base)
                return 0

            lax.fori_loop(1, (most + CHUNK - 1) // CHUNK, more, 0)

    @pl.when(step == steps - 1)
    def _():
        stat_ref[0] = top_ref[...]
        stat_ref[1] = sum_ref[...]


def head_hist(q, w, e_all, tok_all, start, base, scale, nb=1280):
    cols = w.shape[1]
    n = e_all.shape[-1]
    whole = lambda *s: pl.BlockSpec(s, lambda i: (0,) * len(s), pipeline_mode=pl.Buffered(1))
    smem = pl.BlockSpec(memory_space=pltpu.SMEM)
    return pl.pallas_call(
        functools.partial(head_hist_kernel, nb // 256),
        grid=(cols // nb,),
        in_specs=[smem, smem, whole(32, 2048), pl.BlockSpec((2048, nb), lambda i: (0, i)), whole(8, 32, n), whole(8, 64, 128), whole(32, 256)],
        out_specs=[pl.BlockSpec((32, nb), lambda i: (0, i)), pl.BlockSpec((32, nb), lambda i: (0, i)), pl.BlockSpec((2, 32, 128), lambda i: (0, 0, 0))],
        out_shape=[jax.ShapeDtypeStruct((32, cols), F32), jax.ShapeDtypeStruct((32, cols), F32), jax.ShapeDtypeStruct((2, 32, 128), F32)],
        scratch_shapes=[pltpu.VMEM((32, 128), F32), pltpu.VMEM((32, 128), F32)],
        compiler_params=pltpu.CompilerParams(vmem_limit_bytes=VLIM),
        name="head_hist",
    )(start, base, q, w, e_all, tok_all, scale)


def stat_kernel(stat_ref, all_ref, ss, rs):
    s, m = lax.axis_index("store"), lax.axis_index("model")
    barrier = pltpu.get_barrier_semaphore()
    for j in range(1, 4):
        pl.semaphore_signal(barrier, inc=1, device_id=(0, s, lax.rem(m + j, 4)), device_id_type=MESH)
    pl.semaphore_wait(barrier, 3)
    out = [remote(stat_ref, all_ref.at[m], ss.at[j], rs.at[j], s, lax.rem(m + j, 4)) for j in range(1, 4)]
    for c in out:
        c.start()
    all_ref[m] = stat_ref[...]
    for c in out:
        c.wait()


def share_stats(stat):
    vm = pl.BlockSpec(memory_space=pltpu.VMEM)
    return pl.pallas_call(
        stat_kernel, in_specs=[vm], out_specs=vm, out_shape=jax.ShapeDtypeStruct((4, 2, 32, 128), F32),
        scratch_shapes=[pltpu.SemaphoreType.DMA((4,)), pltpu.SemaphoreType.DMA((4,))],
        compiler_params=pltpu.CompilerParams(collective_id=1, has_side_effects=True), name="share_stats",
    )(stat)


def mix_kernel(mix_ref, stat_ref, logit_ref, hist_ref, out_ref):
    tops, sums = stat_ref[:, 0], stat_ref[:, 1]
    top = jnp.max(tops, axis=0)
    total = jnp.sum(sums * jnp.exp(tops - top[None]), axis=0)
    share = ((1.0 - mix_ref[0, 0]) / total)[:, 0:1]
    out_ref[...] = jnp.log(hist_ref[...] + share * jnp.exp(logit_ref[...] - top[:, 0:1]))


def mix(lam, stats, logits, hist, nb=6400):
    rows, cols = logits.shape
    blk = pl.BlockSpec((rows, nb), lambda i: (0, i))
    return pl.pallas_call(
        mix_kernel, grid=(cols // nb,),
        in_specs=[pl.BlockSpec(memory_space=pltpu.SMEM), pl.BlockSpec((4, 2, 32, 128), lambda i: (0, 0, 0, 0)), blk, blk],
        out_specs=blk, out_shape=jax.ShapeDtypeStruct((rows, cols), F32), name="mix",
        compiler_params=pltpu.CompilerParams(vmem_limit_bytes=VLIM),
    )(lam, stats, logits, hist)


def solution(mesh):
    def local_step(queries, w_head, store_keys, store_tok, temperature, mix_weight):
        s, m = lax.axis_index("store"), lax.axis_index("model")
        me = s * 4 + m
        qt = jnp.concatenate([queries, queries], axis=0).T
        tau = temperature.reshape(1, 1)
        lam = mix_weight.reshape(1, 1)
        e, tok, start, stat = scores(qt, store_keys, store_tok.reshape(64, 128), tau)
        e_all, tok_all, start_all, stat_all = exchange(e, tok, start, stat)
        mine = lambda a, own: lax.dynamic_update_slice_in_dim(a, own[None], me, 0)
        e_all = mine(e_all, lax.dynamic_index_in_dim(e, s, 0, keepdims=False)).reshape(8, 32, -1)
        tok_all, start_all = mine(tok_all, tok), mine(start_all, start)
        stat_all = mine(stat_all, lax.dynamic_index_in_dim(stat, s, 0, keepdims=False))
        flat = start_all[:, :, :32].reshape(8, 1024)
        bounds = lax.dynamic_slice_in_dim(flat, m * 250, 251, 1)
        tops = stat_all[:, 0, :, 0]
        up = jnp.exp(tops - jnp.max(tops, axis=0))
        total = jnp.sum(up * stat_all[:, 1, :, 0], axis=0)
        scale = jnp.repeat((mix_weight * up / total).T, CHUNK, axis=1)
        rows = lax.dynamic_slice_in_dim(queries, s * 32, 32, 0)
        base = (m * 64000).astype(I32).reshape(1)
        logits, hist, lm = head_hist(rows, w_head, e_all, tok_all, bounds, base, scale)
        return mix(lam, share_stats(lm), logits, hist)

    group = ("store", "model")
    return jax.shard_map(local_step, mesh=mesh, in_specs=(P("data", None), P(None, "model"), P(group, None), P(group), P(), P()), out_specs=P(("data", "store"), "model"), check_vma=False)
```

profile of v0, /device:TPU:0, one launch (start us, length us, event | category | flops | bytes accessed | tf_op | source)
XLA Modules:
  0.0 266.3 jit_solution(7096223393924912856)
XLA Ops:
  1.3 1.6 constant_dynamic-slice_fusion.q_ref
  2.9 1.2 copy.14
  4.1 1.1 maximum_bitcast_fusion.qt_ref
  5.2 39.3 %scores.1 = (f32[2,4,8,8192]{3,2,1,0:T(8,128)}, s32[64,128]{1,0:T(8,128)}, s32[32,128]{1,0:T(8,128)}, f32[2,2,32,128]{3,2,1,0:T(8,128)}) custom-call(bf16[2048,128]{1,0:T(8,128)(2,1)} %maximum_bitcast_fusion.qt_ref, bf16[8192,2048]{1,0:T(8,128)(2,1)} %keys_ref.1, s32[64,128]{1,0:T(8,128)} %bitcast.18, f32[1,1]{1,0:T(1,128)} %bitcast.14.tau_ref), custom_call_target="tpu_custom_call" | custom-call | tf_op jit(solution)/shard_map/scores/pallas_call | solution.py:110
  44.5 60.9 %exchange.1 = (f32[8,4,8,8192]{3,2,1,0:T(8,128)}, s32[8,64,128]{2,1,0:T(8,128)}, s32[8,32,128]{2,1,0:T(8,128)}, f32[8,2,32,128]{3,2,1,0:T(8,128)}) custom-call(f32[2,4,8,8192]{3,2,1,0:T(8,128)} %get-tuple-element.16.e_ref, s32[64,128]{1,0:T(8,128)} %get-tuple-element.17.tok_ref, s32[32,128]{1,0:T(8,128)} %get-tuple-element.18.start_ref, ...), custom_call_target="tpu_custom_call" | custom-call | tf_op jit(solution)/shard_map/exchange/pallas_call | solution.py:184
  105.4 1.3 bitcast_dynamic-update-slice_fusion.1
  106.7 1.0 reshape.26
  107.7 0.7 constant_dynamic-slice_fusion.1.start_s
  108.4 1.4 dynamic-slice_dynamic-update-slice_fusion.1
  109.8 2.3 dynamic-slice_dynamic-update-slice_fusion
  112.0 1.2 slice_reduce_fusion.1
  113.3 1.4 bitcast_dynamic-update-slice_fusion.tok_ref
  114.7 0.1 copy.16
  114.7 0.1 broadcast_in_dim.15
  114.8 0.7 reshape.29.scale_ref
  115.6 132.8 %head_hist.1 = (f32[32,64000]{1,0:T(8,128)}, f32[32,64000]{1,0:T(8,128)}, f32[2,32,128]{2,1,0:T(8,128)}) custom-call(s32[8,251]{1,0:T(8,128)} %constant_dynamic-slice_fusion.1.start_s, s32[1]{0:T(128)} %bitcast.5.base_s, bf16[32,2048]{1,0:T(8,128)(2,1)} %constant_dynamic-slice_fusion.q_ref, bf16[2048,64000]{1,0:T(8,128)(2,1)} %w_ref.1, ...), custom_call_target="tpu_custom_call" | custom-call | tf_op jit(solution)/shard_map/head_hist/pallas_call | solution.py:279
  248.3 5.5 %share_stats.1.stat_ref = f32[4,2,32,128]{3,2,1,0:T(8,128)} custom-call(f32[2,32,128]{2,1,0:T(8,128)} %get-tuple-element.24.stat_ref), custom_call_target="tpu_custom_call" | custom-call | tf_op jit(solution)/shard_map/share_stats/pallas_call | solution.py:307
  253.8 12.5 %mix.1 = f32[32,64000]{1,0:T(8,128)} custom-call(f32[1,1]{1,0:T(1,128)} %bitcast.15.mix_ref, f32[4,2,32,128]{3,2,1,0:T(8,128)} %share_stats.1.stat_ref, f32[32,64000]{1,0:T(8,128)} %get-tuple-element.25.logit_ref, f32[32,64000]{1,0:T(8,128)} %get-tuple-element.26.hist_ref), custom_call_target="tpu_custom_call" | custom-call | tf_op jit(solution)/shard_map/mix/pallas_call | solution.py:325
  (2 shorter events, 0.0 us)
where the time goes:
time: 269 us; the launch traced here: 266 us
  Pallas kernels  251 us (93%)
  local copies, waits for them, and re-layouts  11.7 us (4%)
    pallas_call x1, Pallas kernels, head_hist(): pl.pallas_call(functools.partial(head_hist_kernel, nb // 256), grid=(cols...  133 us
    pallas_call x1, Pallas kernels, exchange(): pl.pallas_call(exchange_kernel, in_specs=[anyspec] * 4, out_specs=[anyspe...  60.9 us
    pallas_call x1, Pallas kernels, scores(): pl.pallas_call(score_kernel, grid=(n // kb,), in_specs=[whole(2048, 128),...  39.3 us
    pallas_call x1, Pallas kernels, mix(): pl.pallas_call(mix_kernel, grid=(cols // nb,), in_specs=[pl.BlockSpec(mem...  12.5 us
    dynamic_update_slice x4, local copies, waits for them, and re-layouts, local_step(): mine = lambda a, own: lax.dynamic_update_slice_in_dim(a, own[None], me, 0)  6.33 us
    pallas_call x1, Pallas kernels, share_stats(): pl.pallas_call(stat_kernel, in_specs=[vm], out_specs=vm, out_shape=jax.Sh...  5.51 us

commit v1 on v0

v1 whole, which is shorter than its diff:
```python
import functools

import jax
import jax.numpy as jnp
from jax import lax
from jax.experimental import pallas as pl
from jax.experimental.pallas import tpu as pltpu
from jax.sharding import PartitionSpec as P

MESH = pl.DeviceIdType.MESH
F32, BF16, I32 = jnp.float32, jnp.bfloat16, jnp.int32
VLIM = 60 * 1024 * 1024
CHUNK = 32


def iota(shape, dim):
    return lax.broadcasted_iota(I32, shape, dim)


def sort_rows(x):
    n = x.shape[0] * 128
    pos = iota(x.shape, 0) * 128 + iota(x.shape, 1)
    k = 2
    while k <= n:
        j = k // 2
        while j >= 1:
            if j >= 128:
                ahead, behind = pltpu.roll(x, 64 - j // 128, 0), pltpu.roll(x, j // 128, 0)
            else:
                ahead, behind = pltpu.roll(x, 128 - j, 1), pltpu.roll(x, j, 1)
            first = (pos & j) == 0
            other = jnp.where(first, ahead, behind)
            low = ((pos & k) == 0) == first
            x = jnp.where(low, jnp.minimum(x, other), jnp.maximum(x, other))
            j //= 2
        k *= 2
    return x


def score_kernel(qt_ref, keys_ref, tok_ref, tau_ref, e_ref, tok_out, start_out, stat_out, s_ref, top_ref, perm_v, perm_s, hot_a, hot_b, rows_ref, sem):
    step, steps = pl.program_id(0), pl.num_programs(0)
    kb = keys_ref.shape[0]
    sub = 256

    @pl.when(step == 0)
    def _():
        top_ref[...] = jnp.full_like(top_ref, -jnp.inf)
        tok = tok_ref[...]
        packed = sort_rows(tok * 8192 + (iota((64, 128), 0) * 128 + iota((64, 128), 1)))
        tok_out[...] = packed >> 13
        perm_v[...] = packed & 8191
        cp = pltpu.make_async_copy(perm_v, perm_s, sem)
        cp.start()
        for r in range(64):
            tile = tok_ref[r : r + 1, :] >> 8
            lanes = slice(r * 128, (r + 1) * 128)
            hot_a[:, lanes] = jnp.where(iota((32, 128), 0) == (tile >> 5), 1.0, 0.0).astype(BF16)
            hot_b[:, lanes] = jnp.where(iota((128, 128), 0) == (tile & 31), 1.0, 0.0).astype(BF16)
        cnt = lax.dot_general(hot_a[...], hot_b[...], (((1,), (1,)), ((), ())), preferred_element_type=F32)
        inc = cnt
        for sh in (1, 2, 4, 8, 16):
            inc = inc + jnp.where(iota((32, 128), 1) >= sh, pltpu.roll(inc, sh, 1), 0.0)
        tot = jnp.broadcast_to(jnp.sum(cnt, axis=1, keepdims=True), (32, 128))
        rp = tot
        for sh in (1, 2, 4, 8, 16):
            rp = rp + jnp.where(iota((32, 128), 0) >= sh, pltpu.roll(rp, sh, 0), 0.0)
        start_out[...] = ((inc - cnt) + (rp - tot)).astype(I32)
        cp.wait()

    def score(i, _):
        at = pl.multiple_of(i * sub, sub)
        kv = keys_ref[pl.ds(at, sub), :]
        dots = jnp.dot(kv, qt_ref[...], preferred_element_type=F32)
        kf = kv.astype(F32)
        norm = jnp.sum(kf * kf, axis=1, keepdims=True)
        s = (2.0 * dots - norm) / tau_ref[0, 0]
        s_ref[pl.ds(pl.multiple_of(step * kb + at, sub), sub), :] = s
        top_ref[...] = jnp.maximum(top_ref[...], jnp.max(s.reshape(sub // 8, 8, 128), axis=0))
        return 0

    lax.fori_loop(0, kb // sub, score, 0)

    @pl.when(step == steps - 1)
    def _():
        top = jnp.max(top_ref[...], axis=0, keepdims=True)

        def block(b, total):
            for u in range(128):
                rows_ref[u : u + 1, :] = s_ref[pl.ds(perm_s[b, u], 1), :]
            x = jnp.exp(rows_ref[...] - top)
            total = total + jnp.sum(x.reshape(16, 8, 128), axis=0)
            xt = x.T
            lanes = pl.ds(pl.multiple_of(b * 128, 128), 128)
            for g in range(8):
                e_ref[g // 4, g % 4, :, lanes] = xt[8 * g : 8 * g + 8, :]
            return total

        total = lax.fori_loop(0, 64, block, jnp.zeros((8, 128), F32))
        total = jnp.sum(total, axis=0, keepdims=True)
        mt = jnp.broadcast_to(top, (128, 128)).T
        zt = jnp.broadcast_to(total, (128, 128)).T
        for s in range(2):
            stat_out[s, 0] = mt[32 * s : 32 * s + 32]
            stat_out[s, 1] = zt[32 * s : 32 * s + 32]


def scores(qt, keys, tok, tau, kb=1024):
    n = keys.shape[0]
    whole = lambda *s: pl.BlockSpec(s, lambda i: (0,) * len(s))
    return pl.pallas_call(
        score_kernel,
        grid=(n // kb,),
        in_specs=[whole(2048, 128), pl.BlockSpec((kb, 2048), lambda i: (i, 0)), whole(64, 128), pl.BlockSpec(memory_space=pltpu.SMEM)],
        out_specs=[whole(2, 4, 8, n), whole(64, 128), whole(32, 128), whole(2, 2, 32, 128)],
        out_shape=[jax.ShapeDtypeStruct((2, 4, 8, n), F32), jax.ShapeDtypeStruct((64, 128), I32), jax.ShapeDtypeStruct((32, 128), I32), jax.ShapeDtypeStruct((2, 2, 32, 128), F32)],
        scratch_shapes=[
            pltpu.VMEM((n, 128), F32), pltpu.VMEM((8, 128), F32), pltpu.VMEM((64, 128), I32), pltpu.SMEM((64, 128), I32),
            pltpu.VMEM((32, n), BF16), pltpu.VMEM((128, n), BF16), pltpu.VMEM((128, 128), F32), pltpu.SemaphoreType.DMA,
        ],
        compiler_params=pltpu.CompilerParams(vmem_limit_bytes=VLIM),
        name="scores",
    )(qt, keys, tok, tau)


def peers():
    s, m = lax.axis_index("store"), lax.axis_index("model")
    x, c = m // 2, m % 2
    return s, m, 1 - s, (1 - x) * 2 + c, x * 2 + (1 - c)


def remote(src, dst, ss, rs, s, m):
    return pltpu.make_async_remote_copy(src_ref=src, dst_ref=dst, send_sem=ss, recv_sem=rs, device_id=(0, s, m), device_id_type=MESH)


def window(e_ref, tok_ref, starts, ends=None):
    lane, lane1 = iota((32, 128), 1), iota((1, 128), 1)
    halves, toks = [], []
    for h in range(2):
        acc, tacc = None, None
        for i in range(4):
            d = 4 * h + i
            at = starts[d]
            row, off = jnp.minimum(at >> 7, 63), at & 127
            nxt = jnp.minimum(row + 1, 63)
            v0 = e_ref[d, :, :, pl.ds(pl.multiple_of(row * 128, 128), 128)].reshape(32, 128)
            v1 = e_ref[d, :, :, pl.ds(pl.multiple_of(nxt * 128, 128), 128)].reshape(32, 128)
            sh = (CHUNK * i - off) & 127
            v = pltpu.roll(jnp.where(lane >= off, v0, v1), sh, 1)
            t0, t1 = tok_ref[d, pl.ds(row, 1), :], tok_ref[d, pl.ds(nxt, 1), :]
            t = pltpu.roll(jnp.where(lane1 >= off, t0, t1), sh, 1)
            if ends is not None:
                t = jnp.where(lane1 - CHUNK * i < ends[d] - at, t, -1)
            if i == 0:
                acc, tacc = v, t
            else:
                acc = jnp.where(lane >= CHUNK * i, v, acc)
                tacc = jnp.where(lane1 >= CHUNK * i, t, tacc)
        halves.append(acc)
        toks.append(tacc)
    return jnp.concatenate(halves, axis=1), jnp.concatenate(toks, axis=1)


def product(e, tok):
    hi = e.astype(BF16)
    rest = e - hi.astype(F32)
    mid = rest.astype(BF16)
    low = (rest - mid.astype(F32)).astype(BF16)
    lhs = jnp.concatenate([hi, mid, low], axis=0)
    hot = jnp.where(iota((256, 256), 0) == tok, 1.0, 0.0).astype(BF16)
    out = lax.dot_general(lhs, hot, (((1,), (1,)), ((), ())), preferred_element_type=F32)
    return out[0:32] + out[32:64] + out[64:96]


def source_scale(stat_ref, lam):
    tops = stat_ref[:, 0]
    up = jnp.exp(tops - jnp.max(tops, axis=0)[None])
    total = jnp.sum(up * stat_ref[:, 1], axis=0)
    up = up * (lam / total)[None]
    lane = iota((32, 128), 1)
    halves = []
    for h in range(2):
        acc = up[4 * h]
        for i in range(1, 4):
            acc = jnp.where(lane >= CHUNK * i, up[4 * h + i], acc)
        halves.append(acc)
    return jnp.concatenate(halves, axis=1)


NB = 512
NBUF = 10
TRIPS = 25
TILES = 10
PER = 2
WIDE = TILES * 256


class Head:
    def __init__(self, first, last, s, q_ref, w_ref, logit_ref, w_buf, l_buf, top_ref, sum_ref, w_sem, l_sem):
        self.__dict__.update({k: v for k, v in locals().items() if k != "self"})

    def w_copy(self, i):
        slot = lax.rem(i, NBUF)
        cols = pl.ds(pl.multiple_of((self.first + i) * NB, NB), NB)
        return pltpu.make_async_copy(self.w_ref.at[:, cols], self.w_buf.at[slot], self.w_sem.at[slot])

    def l_copy(self, i):
        slot = lax.rem(i, 2)
        cols = pl.ds(pl.multiple_of(i * NB, NB), NB)
        return pltpu.make_async_copy(self.l_buf.at[slot], self.logit_ref.at[:, cols], self.l_sem.at[slot])

    def prime(self):
        for i in range(NBUF - 2):
            self.w_copy(i).start()

    def enter(self, i):
        @pl.when(i + NBUF - 2 < self.last - self.first)
        def _():
            self.w_copy(i + NBUF - 2).start()

        @pl.when(i >= 2)
        def _():
            self.l_copy(i - 2).wait()

        self.w_copy(i).wait()

    def logits(self, i):
        out = jnp.dot(self.q_ref[self.s], self.w_buf[lax.rem(i, NBUF)], preferred_element_type=F32)
        self.l_buf[lax.rem(i, 2)] = out
        old = self.top_ref[...]
        new = jnp.maximum(old, jnp.max(out, axis=1, keepdims=True))
        self.sum_ref[...] = self.sum_ref[...] * jnp.exp(old - new) + jnp.sum(jnp.exp(out - new[:, 0:1]), axis=1, keepdims=True)
        self.top_ref[...] = new

    def drain(self):
        for i in (2, 1):
            self.l_copy(self.last - self.first - i).wait()

    def run(self, lo, hi):
        def one(i, _):
            self.enter(i)
            self.logits(i)
            self.l_copy(i).start()
            return 0

        lax.fori_loop(lo, hi, one, 0)


def head_scratch():
    dma = pltpu.SemaphoreType.DMA
    return [pltpu.VMEM((NBUF, 2048, NB), BF16), pltpu.VMEM((2, 32, NB), F32), pltpu.VMEM((32, 128), F32), pltpu.VMEM((32, 128), F32), dma((NBUF,)), dma((2,))]


def exchange_kernel(first, last, q_ref, e_ref, tok_ref, start_ref, stat_ref, w_ref,
                    logit_ref, e_all, tok_all, start_all, stat_all, lm_ref,
                    w_buf, l_buf, top_ref, sum_ref, w_sem, l_sem, loc_sem, es, er, ps, pr, ts, tr):
    s, m, so, mx, mc = peers()
    me = s * 4 + m
    head = Head(first, last, s, q_ref, w_ref, logit_ref, w_buf, l_buf, top_ref, sum_ref, w_sem, l_sem)
    head.prime()

    barrier = pltpu.get_barrier_semaphore()
    for j in range(1, 8):
        d = lax.rem(me + j, 8)
        pl.semaphore_signal(barrier, inc=1, device_id=(0, d // 4, lax.rem(d, 4)), device_id_type=MESH)
    pl.semaphore_wait(barrier, 7)

    far = []
    for r in range(4):
        far.append([
            remote(e_ref.at[so, r], e_all.at[me, r], es.at[0, r], er.at[0, r], so, mx),
            remote(e_ref.at[s, r], e_all.at[me, r], es.at[1, r], er.at[1, r], s, mx),
            remote(e_ref.at[so, r], e_all.at[me, r], es.at[2, r], er.at[2, r], so, m),
        ])
        for c in far[-1]:
            c.start()
    own = [remote(e_ref.at[s, r], e_all.at[me, r], ps.at[3, r], pr.at[3, r], s, mc) for r in range(4)]
    for c in own:
        c.start()
    small = []
    for j in range(1, 8):
        d = lax.rem(me + j, 8)
        ds_, dm = d // 4, lax.rem(d, 4)
        for k, (a, b) in enumerate(((tok_ref, tok_all.at[me]), (start_ref, start_all.at[me]), (stat_ref.at[ds_], stat_all.at[me]))):
            small.append(remote(a, b, ts.at[j, k], tr.at[j, k], ds_, dm))
    for c in small:
        c.start()
    mine = pltpu.make_async_copy(e_ref.at[s], e_all.at[me], loc_sem)
    mine.start()
    tok_all[me] = tok_ref[...]
    start_all[me] = start_ref[...]
    stat_all[me] = stat_ref[s]
    top_ref[...] = jnp.full_like(top_ref, -jnp.inf)
    sum_ref[...] = jnp.zeros_like(sum_ref)

    came = (so * 4 + mx, s * 4 + mx, so * 4 + m)
    blocks = last - first
    fwd = []
    for r in range(4):
        head.run(r * blocks // 4, (r + 1) * blocks // 4)
        for k in (1, 2, 0):
            far[r][k].wait_recv()
            f = remote(e_all.at[came[k], r], e_all.at[came[k], r], ps.at[k, r], pr.at[k, r], s, mc)
            f.start()
            fwd.append(f)
    head.drain()
    lm_ref[0] = top_ref[...]
    lm_ref[1] = sum_ref[...]
    mine.wait()
    for c in own + fwd + small:
        c.wait()
    for r in range(4):
        for c in far[r]:
            c.wait_send()


def exchange(first, last, q, e, tok, start, stat, w):
    n = e.shape[-1]
    anyspec, vm = pl.BlockSpec(memory_space=pl.ANY), pl.BlockSpec(memory_space=pltpu.VMEM)
    dma = pltpu.SemaphoreType.DMA
    return pl.pallas_call(
        functools.partial(exchange_kernel, first, last),
        in_specs=[vm, anyspec, vm, vm, vm, anyspec],
        out_specs=[anyspec, anyspec, vm, vm, vm, vm],
        out_shape=[
            jax.ShapeDtypeStruct((32, (last - first) * NB), F32), jax.ShapeDtypeStruct((8, 4, 8, n), F32),
            jax.ShapeDtypeStruct((8, 64, 128), I32), jax.ShapeDtypeStruct((8, 32, 128), I32), jax.ShapeDtypeStruct((8, 2, 32, 128), F32),
            jax.ShapeDtypeStruct((2, 32, 128), F32),
        ],
        scratch_shapes=head_scratch() + [dma, dma((3, 4)), dma((3, 4)), dma((4, 4)), dma((4, 4)), dma((8, 3)), dma((8, 3))],
        compiler_params=pltpu.CompilerParams(collective_id=0, has_side_effects=True, vmem_limit_bytes=VLIM),
        name="exchange",
    )(q, e, tok, start, stat, w)


def hist_kernel(first, last, pos_ref, lam_ref, start_s, q_ref, start_ref, tok_ref, stat_ref, lm_in, e_hbm, w_ref,
                logit_ref, hist_ref, lm_ref,
                e_ref, h_buf, scale_ref, wide_ref, h_sem, e_sem, w_buf, l_buf, top_ref, sum_ref, w_sem, l_sem):
    s, m = pos_ref[0], pos_ref[1]
    head = Head(first, last, s, q_ref, w_ref, logit_ref, w_buf, l_buf, top_ref, sum_ref, w_sem, l_sem)
    load = pltpu.make_async_copy(e_hbm, e_ref, e_sem)
    load.start()
    head.prime()
    top_ref[...] = lm_in[0]
    sum_ref[...] = lm_in[1]
    scale_ref[...] = source_scale(stat_ref, lam_ref[0, 0])
    low = m * (TRIPS * TILES)
    tile = iota((32, 128), 0) * 32 + iota((32, 128), 1)
    inside = (iota((32, 128), 1) < 32) & (tile >= low) & (tile < low + TRIPS * TILES)
    wide = jnp.zeros((32, 128), I32)
    for d in range(8):
        a = start_ref[d]
        below = jnp.broadcast_to(pltpu.roll(a, 31, 0)[:, 0:1], (32, 128))
        b = jnp.where(iota((32, 128), 1) == 31, below, pltpu.roll(a, 127, 1))
        wide = jnp.maximum(wide, jnp.where(inside, b - a, 0))
    wide_ref[0] = jnp.max(wide)
    load.wait()

    def h_copy(j):
        slot = lax.rem(j, 2)
        return pltpu.make_async_copy(h_buf.at[slot], hist_ref.at[:, pl.ds(pl.multiple_of(j * WIDE, 256), WIDE)], h_sem.at[slot])

    def edges(g):
        return [start_s[d, g >> 5, g & 31] for d in range(8)]

    def trip(j, _):
        for i in range(PER):
            head.enter(PER * j + i)

        @pl.when(j >= 2)
        def _():
            h_copy(j - 2).wait()

        slot = lax.rem(j, 2)
        scale = scale_ref[...]
        g0 = low + j * TILES
        for i in range(PER):
            head.logits(PER * j + i)
        for i in range(TILES):
            e, tok = window(e_ref, tok_ref, edges(g0 + i))
            h_buf[slot, :, i * 256 : (i + 1) * 256] = product(e * scale, tok - (g0 + i) * 256)
        for i in range(PER):
            head.l_copy(PER * j + i).start()

        @pl.when(wide_ref[0] > CHUNK)
        def _():
            def extra(i, _):
                starts, ends = edges(g0 + i), edges(g0 + i + 1)
                most = functools.reduce(jnp.maximum, [b - a for a, b in zip(starts, ends)])
                cols = pl.ds(pl.multiple_of(i * 256, 256), 256)

                def more(it, _):
                    at = [jnp.minimum(a + it * CHUNK, b) for a, b in zip(starts, ends)]
                    e, tok = window(e_ref, tok_ref, at, ends)
                    h_buf[slot, :, cols] += product(e * scale_ref[...], tok - (g0 + i) * 256)
                    return 0

                lax.fori_loop(1, (most + CHUNK - 1) // CHUNK, more, 0)
                return 0

            lax.fori_loop(0, TILES, extra, 0)

        h_copy(j).start()
        return 0

    lax.fori_loop(0, TRIPS, trip, 0)
    lm_ref[0] = top_ref[...]
    lm_ref[1] = sum_ref[...]
    head.drain()
    for i in (2, 1):
        h_copy(TRIPS - i).wait()


def hist_head(first, last, pos, lam, q, start, tok, stat, lm, e_all, w):
    cols = w.shape[1]
    anyspec, vm, sm = (pl.BlockSpec(memory_space=k) for k in (pl.ANY, pltpu.VMEM, pltpu.SMEM))
    dma = pltpu.SemaphoreType.DMA
    return pl.pallas_call(
        functools.partial(hist_kernel, first, last),
        in_specs=[sm, sm, sm, vm, vm, vm, vm, vm, anyspec, anyspec],
        out_specs=[anyspec, anyspec, vm],
        out_shape=[jax.ShapeDtypeStruct((32, (last - first) * NB), F32), jax.ShapeDtypeStruct((32, cols), F32), jax.ShapeDtypeStruct((2, 32, 128), F32)],
        scratch_shapes=[pltpu.VMEM(e_all.shape, F32), pltpu.VMEM((2, 32, WIDE), F32), pltpu.VMEM((32, 256), F32), pltpu.SMEM((1,), I32), dma((2,)), dma] + head_scratch(),
        compiler_params=pltpu.CompilerParams(vmem_limit_bytes=VLIM),
        name="hist_head",
    )(pos, lam, start, q, start, tok, stat, lm, e_all, w)


def stat_kernel(stat_ref, all_ref, ss, rs):
    s, m = lax.axis_index("store"), lax.axis_index("model")
    barrier = pltpu.get_barrier_semaphore()
    for j in range(1, 4):
        pl.semaphore_signal(barrier, inc=1, device_id=(0, s, lax.rem(m + j, 4)), device_id_type=MESH)
    pl.semaphore_wait(barrier, 3)
    out = [remote(stat_ref, all_ref.at[m], ss.at[j], rs.at[j], s, lax.rem(m + j, 4)) for j in range(1, 4)]
    for c in out:
        c.start()
    all_ref[m] = stat_ref[...]
    for c in out:
        c.wait()


def share_stats(stat):
    vm = pl.BlockSpec(memory_space=pltpu.VMEM)
    return pl.pallas_call(
        stat_kernel, in_specs=[vm], out_specs=vm, out_shape=jax.ShapeDtypeStruct((4, 2, 32, 128), F32),
        scratch_shapes=[pltpu.SemaphoreType.DMA((4,)), pltpu.SemaphoreType.DMA((4,))],
        compiler_params=pltpu.CompilerParams(collective_id=1, has_side_effects=True), name="share_stats",
    )(stat)


def mix_kernel(cuts, lam_ref, stat_ref, *refs):
    parts, hist_ref, out_ref = refs[:-2], refs[-2], refs[-1]
    tops, sums = stat_ref[:, 0], stat_ref[:, 1]
    top = jnp.max(tops, axis=0)
    total = jnp.sum(sums * jnp.exp(tops - top[None]), axis=0)
    share = ((1.0 - lam_ref[0, 0]) / total)[:, 0:1]
    step = pl.program_id(0)
    for k, ref in enumerate(parts):
        @pl.when((step >= cuts[k]) & (step < cuts[k + 1]))
        def _():
            out_ref[...] = jnp.log(hist_ref[...] + share * jnp.exp(ref[...] - top[:, 0:1]))


def mix(lam, stats, parts, hist, nb=6400):
    rows, cols = hist.shape
    blk = pl.BlockSpec((rows, nb), lambda i: (0, i))
    cuts = [0]
    for p in parts:
        cuts.append(cuts[-1] + p.shape[1] // nb)
    part = lambda k: pl.BlockSpec((rows, nb), lambda i: (0, jnp.clip(i - cuts[k], 0, cuts[k + 1] - cuts[k] - 1)))
    return pl.pallas_call(
        functools.partial(mix_kernel, tuple(cuts)), grid=(cols // nb,),
        in_specs=[pl.BlockSpec(memory_space=pltpu.SMEM), pl.BlockSpec((4, 2, 32, 128), lambda i: (0, 0, 0, 0))] + [part(k) for k in range(len(parts))] + [blk],
        out_specs=blk, out_shape=jax.ShapeDtypeStruct((rows, cols), F32), name="mix",
        compiler_params=pltpu.CompilerParams(vmem_limit_bytes=VLIM),
    )(lam, stats, *parts, hist)


def solution(mesh):
    def local_step(queries, w_head, store_keys, store_tok, temperature, mix_weight):
        s, m = lax.axis_index("store"), lax.axis_index("model")
        blocks = w_head.shape[1] // NB
        cut = blocks - PER * TRIPS
        qt = jnp.concatenate([queries, queries], axis=0).T
        tau = temperature.reshape(1, 1)
        lam = mix_weight.reshape(1, 1)
        q = queries.reshape(2, 32, -1)
        e, tok, start, stat = scores(qt, store_keys, store_tok.reshape(64, 128), tau)
        la, e_all, tok_all, start_all, stat_all, lm = exchange(0, cut, q, e, tok, start, stat, w_head)
        pos = jnp.stack([s, m]).astype(I32)
        lb, hist, lm = hist_head(cut, blocks, pos, lam, q, start_all, tok_all, stat_all, lm, e_all, w_head)
        return mix(lam, share_stats(lm), [la, lb], hist)

    group = ("store", "model")
    return jax.shard_map(local_step, mesh=mesh, in_specs=(P("data", None), P(None, "model"), P(group, None), P(group), P(), P()), out_specs=P(("data", "store"), "model"), check_vma=False)
```

time: 269 us -> 183 us (0.68)
  Pallas kernels: 251 us -> 178 us
  local copies, waits for them, and re-layouts: 11.7 us -> 1.22 us
    pallas_call x3, Pallas kernels: 206 us -> 133 us  [the longest x1 64.4 us: exchange(): pl.pallas_call(functools.partial(exchange_kernel, first, last), in_specs=...]
    dynamic_update_slice x4 -> x0, local copies, waits for them, and re-layouts: 6.33 us -> none  [local_step(): mine = lambda a, own: lax.dynamic_update_slice_in_dim(a, own[None], me, 0)]
where the time goes in v1:
time: 183 us; the launch traced here: 182 us
  Pallas kernels  178 us (97%)
    pallas_call x1, Pallas kernels, exchange(): pl.pallas_call(functools.partial(exchange_kernel, first, last), in_specs=...  64.4 us
    pallas_call x1, Pallas kernels, hist_head(): pl.pallas_call(functools.partial(hist_kernel, first, last), in_specs=[sm,...  56.4 us
    pallas_call x1, Pallas kernels, scores(): pl.pallas_call(score_kernel, grid=(n // kb,), in_specs=[whole(2048, 128),...  39.3 us
    pallas_call x1, Pallas kernels, mix(): pl.pallas_call(functools.partial(mix_kernel, tuple(cuts)), grid=(cols //...  12.4 us
    pallas_call x1, Pallas kernels, share_stats(): pl.pallas_call(stat_kernel, in_specs=[vm], out_specs=vm, out_shape=jax.Sh...  5.52 us

profile of v1, /device:TPU:0, one launch (start us, length us, event | category | flops | bytes accessed | tf_op | source)
XLA Modules:
  0.0 182.2 jit_solution(18364383543661899467)
XLA Ops:
  1.3 0.6 pad_add_fusion.pos_ref
  1.9 1.2 copy.7
  3.1 1.1 maximum_bitcast_fusion.qt_ref
  4.2 39.3 %scores.1 = (f32[2,4,8,8192]{3,2,1,0:T(8,128)}, s32[64,128]{1,0:T(8,128)}, s32[32,128]{1,0:T(8,128)}, f32[2,2,32,128]{3,2,1,0:T(8,128)}) custom-call(bf16[2048,128]{1,0:T(8,128)(2,1)} %maximum_bitcast_fusion.qt_ref, bf16[8192,2048]{1,0:T(8,128)(2,1)} %keys_ref.1, s32[64,128]{1,0:T(8,128)} %bitcast.13, f32[1,1]{1,0:T(1,128)} %bitcast.8.tau_ref), custom_call_target="tpu_custom_call" | custom-call | tf_op jit(solution)/shard_map/scores/pallas_call | solution.py:110
  43.5 64.4 %exchange.1 = (f32[32,38400]{1,0:T(8,128)}, f32[8,4,8,8192]{3,2,1,0:T(8,128)}, s32[8,64,128]{2,1,0:T(8,128)}, s32[8,32,128]{2,1,0:T(8,128)}, f32[8,2,32,128]{3,2,1,0:T(8,128)}, /*index=5*/f32[2,32,128]{2,1,0:T(8,128)}) custom-call(bf16[2,32,2048]{2,1,0:T(8,128)(2,1)} %bitcast.11, f32[2,4,8,8192]{3,2,1,0:T(8,128)} %get-tuple-element.18.e_ref, ...), custom_call_target="tpu_custom_call" | custom-call | tf_op jit(solution)/shard_map/exchange/pallas_call | solution.py:320
  107.8 56.4 %hist_head.1 = (f32[32,25600]{1,0:T(8,128)}, f32[32,64000]{1,0:T(8,128)}, f32[2,32,128]{2,1,0:T(8,128)}) custom-call(s32[2]{0:T(128)} %pad_add_fusion.pos_ref, f32[1,1]{1,0:T(1,128)} %bitcast.9.lam_ref, s32[8,32,128]{2,1,0:T(8,128)} %get-tuple-element.22.start_s.start_ref, bf16[2,32,2048]{2,1,0:T(8,128)(2,1)} %bitcast.12, ...), custom_call_target="tpu_custom_call" | custom-call | tf_op jit(solution)/shard_map/hist_head/pallas_call | solution.py:417
  164.3 5.5 %share_stats.1.stat_ref = f32[4,2,32,128]{3,2,1,0:T(8,128)} custom-call(f32[2,32,128]{2,1,0:T(8,128)} %get-tuple-element.27.stat_ref), custom_call_target="tpu_custom_call" | custom-call | tf_op jit(solution)/shard_map/share_stats/pallas_call | solution.py:444
  169.8 12.4 %mix.1 = f32[32,64000]{1,0:T(8,128)} custom-call(f32[1,1]{1,0:T(1,128)} %bitcast.10.lam_ref, f32[4,2,32,128]{3,2,1,0:T(8,128)} %share_stats.1.stat_ref, f32[32,38400]{1,0:T(8,128)} %get-tuple-element.28.refs_0_, f32[32,25600]{1,0:T(8,128)} %get-tuple-element.29.refs_1_, f32[32,64000]{1,0:T(8,128)} %get-tuple-element.30.refs_2_), custom_call_target="tpu_custom_call" | custom-call | tf_op jit(solution)/shard_map/mix/pallas_call | solution.py:471
